TPU v7x, 8 devices: a whole 2x2x1 slice. The times are simulated.
8 devices in a mesh: rep: 2 (over z, y), ep: 4 (over x, core).
Axes of the slice: x: 2, y: 2, z: 1, core: 2. Of those that a mesh axis runs over, the one named last changes fastest.
Arguments:
- x: bfloat16 [1024, 2048], P(('rep', 'ep')), parts along dimension 0
- cache: bfloat16 [1024, 256, 576], P(('rep', 'ep')), parts along dimension 0
- lens: int32 [1024], P(('rep', 'ep')), parts along dimension 0
- ids: int32 [1024, 6], P(('rep', 'ep')), parts along dimension 0
- rw: float32 [1024, 6], P(('rep', 'ep')), parts along dimension 0
- w_q: bfloat16 [2048, 3072], replicated
- w_dkv: bfloat16 [2048, 576], replicated
- w_uk: bfloat16 [16, 128, 512], replicated
- w_uv: bfloat16 [16, 512, 128], replicated
- w_o: bfloat16 [2048, 2048], replicated
- s_gate: bfloat16 [2048, 2816], replicated
- s_up: bfloat16 [2048, 2816], replicated
- s_down: bfloat16 [2816, 2048], replicated
- e_gate: bfloat16 [64, 2048, 1408], P('ep')
- e_up: bfloat16 [64, 2048, 1408], P('ep')
- e_down: bfloat16 [64, 1408, 2048], P('ep')
Outputs:
- output 1: bfloat16 [1024, 2048], P(('rep', 'ep')), parts along dimension 0
- output 2: bfloat16 [1024, 576], P(('rep', 'ep')), parts along dimension 0
There are 2 independent parts. A program takes and returns all parts, laid end to end along the dimension named above; an argument that names none is the same for every part.
All inputs are finite; a program needn't handle non-finite values.
Results may differ from a plain program's by a relative error of at most 0.0118975.
Values are sent between devices in bfloat16 or wider.
A program may use at most 1.5 GiB of HBM per device.

v0:
```python
import jax
import jax.numpy as jnp
from jax import lax
from jax.sharding import PartitionSpec as P, NamedSharding

EPS = 1e-6
ROPE_BASE = 1.0e4
CAP_FACTOR = 2


def rms(v):
    v = v.astype(jnp.float32)
    return v * lax.rsqrt(jnp.mean(v * v, axis=-1, keepdims=True) + EPS)


def rope(v, pos):
    half = v.shape[-1] // 2
    inv = ROPE_BASE ** (-2.0 * jnp.arange(half, dtype=jnp.float32) / v.shape[-1])
    ang = pos.astype(jnp.float32)[..., None] * inv
    cs = jnp.cos(ang)
    sn = jnp.sin(ang)
    v1 = v[..., :half]
    v2 = v[..., half:]
    return jnp.concatenate([v1 * cs - v2 * sn, v2 * cs + v1 * sn], axis=-1)


def swiglu(u, wg, wu, wd):
    g = jnp.dot(u, wg, preferred_element_type=jnp.float32)
    v = jnp.dot(u, wu, preferred_element_type=jnp.float32)
    return jnp.dot((jax.nn.silu(g) * v).astype(jnp.bfloat16), wd, preferred_element_type=jnp.float32)


def route(col, w, n_col, cap):
    bsz, top = col.shape
    hit = (col[:, :, None] == jnp.arange(n_col)[None, None, :]).astype(jnp.bfloat16)
    flat = hit.reshape(bsz * top, n_col)
    idx = jnp.arange(bsz * top)
    low = (idx[:, None] > idx[None, :]).astype(jnp.bfloat16)
    before = jnp.dot(low, flat, preferred_element_type=jnp.float32)
    rank = jnp.sum(before * flat.astype(jnp.float32), axis=1).astype(jnp.int32).reshape(bsz, top)
    at = (rank[:, :, None] == jnp.arange(cap)[None, None, :]).astype(jnp.bfloat16)
    disp = jnp.einsum('bke,bkr->ber', hit, at, preferred_element_type=jnp.float32).astype(jnp.bfloat16).reshape(bsz, n_col * cap)
    w = w.astype(jnp.float32)
    w1 = w.astype(jnp.bfloat16)
    r1 = w - w1.astype(jnp.float32)
    w2 = r1.astype(jnp.bfloat16)
    w3 = (r1 - w2.astype(jnp.float32)).astype(jnp.bfloat16)
    hw = jnp.stack([w1, w2, w3])[:, :, :, None] * hit[None]
    comb = jnp.einsum('jbke,bkr->jber', hw, at, preferred_element_type=jnp.float32).astype(jnp.bfloat16).reshape(-1, n_col * cap)
    return disp, comb


def attention(x, cache, lens, w_q, w_dkv, w_uk, w_uv, w_o):
    bsz = x.shape[0]
    heads, nope, kvl = w_uk.shape
    kvd = cache.shape[2]
    vh = w_uv.shape[2]
    qkd = nope + kvd - kvl
    xn = rms(x).astype(jnp.bfloat16)
    q = jnp.dot(xn, w_q, preferred_element_type=jnp.float32).astype(jnp.bfloat16).reshape(bsz, heads, qkd)
    kv = jnp.dot(xn, w_dkv, preferred_element_type=jnp.float32)
    kv_new = jnp.concatenate([rms(kv[:, :kvl]), rope(kv[:, kvl:], lens)], axis=-1).astype(jnp.bfloat16)
    q_lat = jnp.einsum('bhd,hdc->bhc', q[:, :, :nope], w_uk, preferred_element_type=jnp.float32).astype(jnp.bfloat16)
    q_rot = rope(q[:, :, nope:].astype(jnp.float32), lens[:, None]).astype(jnp.bfloat16)
    qf = jnp.concatenate([q_lat, q_rot], axis=-1)
    scale = qkd ** -0.5
    s = jnp.einsum('bhc,blc->bhl', qf, cache, preferred_element_type=jnp.float32) * scale
    live = jnp.arange(cache.shape[1])[None, None, :] < lens[:, None, None]
    s = jnp.where(live, s, -jnp.inf)
    s_new = jnp.einsum('bhc,bc->bh', qf, kv_new, preferred_element_type=jnp.float32) * scale
    mx = jnp.maximum(jnp.max(s, axis=2), s_new)
    e = jnp.exp(s - mx[:, :, None])
    e_new = jnp.exp(s_new - mx)
    den = jnp.sum(e, axis=2) + e_new
    p = (e / den[:, :, None]).astype(jnp.bfloat16)
    p_new = (e_new / den).astype(jnp.bfloat16)
    o_all = jnp.einsum('bhl,blc->bhc', p, cache, preferred_element_type=jnp.float32)
    o_lat = (o_all[:, :, :kvl] + p_new.astype(jnp.float32)[:, :, None] * kv_new[:, None, :kvl].astype(jnp.float32)).astype(jnp.bfloat16)
    o = jnp.einsum('bhc,hcv->bhv', o_lat, w_uv, preferred_element_type=jnp.float32).astype(jnp.bfloat16).reshape(bsz, heads * vh)
    a = jnp.dot(o, w_o, preferred_element_type=jnp.float32)
    return (x.astype(jnp.float32) + a).astype(jnp.bfloat16), kv_new


def solution(mesh):
    n = mesh.shape['ep']
    tok_spec = P(('rep', 'ep'))
    row_spec = P(('rep', 'ep'), None)
    cache_spec = P(('rep', 'ep'), None, None)
    exp_spec = P('ep', None, None)

    def local(x, cache, lens, ids, rw, w_q, w_dkv, w_uk, w_uv, w_o, s_gate, s_up, s_down, e_gate, e_up, e_down):
        h1, kv_new = attention(x, cache, lens, w_q, w_dkv, w_uk, w_uv, w_o)
        u = rms(h1).astype(jnp.bfloat16)
        shared = swiglu(u, s_gate, s_up, s_down)
        b_dev, top = ids.shape
        hid = x.shape[1]
        e_loc = e_gate.shape[0]
        n_exp = e_loc * n
        cape = (CAP_FACTOR * b_dev * top + n_exp - 1) // n_exp
        disp, comb = route(ids, rw, n_exp, cape)
        send = jnp.einsum('br,bh->rh', disp, u, preferred_element_type=jnp.float32).astype(jnp.bfloat16)
        recv = lax.all_to_all(send, 'ep', 0, 0, tiled=True)
        xr = recv.reshape(n, e_loc, cape, hid).transpose(1, 0, 2, 3).reshape(e_loc, n * cape, hid)
        g = jnp.einsum('erh,ehi->eri', xr, e_gate, preferred_element_type=jnp.float32)
        v = jnp.einsum('erh,ehi->eri', xr, e_up, preferred_element_type=jnp.float32)
        act = (jax.nn.silu(g) * v).astype(jnp.bfloat16)
        out = jnp.einsum('eri,eih->erh', act, e_down, preferred_element_type=jnp.float32).astype(jnp.bfloat16)
        back = out.reshape(e_loc, n, cape, hid).transpose(1, 0, 2, 3).reshape(n_exp * cape, hid)
        ret = lax.all_to_all(back, 'ep', 0, 0, tiled=True)
        routed = jnp.dot(comb, ret, preferred_element_type=jnp.float32).reshape(-1, b_dev, hid).sum(axis=0)
        y = (h1.astype(jnp.float32) + shared + routed).astype(jnp.bfloat16)
        return y, kv_new

    in_specs = (row_spec, cache_spec, tok_spec, row_spec, row_spec) + (P(),) * 8 + (exp_spec,) * 3
    return jax.shard_map(local, mesh=mesh, in_specs=in_specs, out_specs=(row_spec, row_spec), check_vma=False)
```

profile of v0, /device:TPU:0, one launch (start us, length us, event | category | flops | bytes accessed | tf_op | source)
XLA Modules:
  0.0 349.6 jit_solution(2019585069692442843)
XLA Ops:
  0.7 0.8 convert_element_type.128
  1.5 0.8 iota_compare_fusion.12
  2.3 1.2 fusion.21
  3.5 1.9 fusion.38
  5.4 0.1 multiply_reduce_fusion.2
  5.5 0.8 copy.77
  6.4 0.1 multiply_cosine_fusion
  6.5 0.1 copy.97
  6.7 0.1 copy.69
  6.8 0.4 copy-done.5
  7.2 0.1 copy.70
  7.3 6.5 %convolution_convert_fusion.2 = bf16[128,3072]{1,0:T(8,128)(2,1)S(1)} fusion(bf16[2048,3072]{1,0:T(8,128)(2,1)} %param.21, bf16[128,2048]{1,0:T(8,128)(2,1)S(1)} %copy-done.2, f32[128]{0:T(128)S(1)} %add_rsqrt_fusion.2), kind=kOutput, calls=%fused_computation.8 | convolution fusion | flops 1611792384 | bytes 13894144 | tf_op jit(solution)/shard_map/dot_general | solution.py:60
  13.8 0.4 copy.66
  14.2 0.3 copy.96
  14.5 0.1 convert_element_type.127
  14.6 2.3 convert_bitcast_fusion.1
  16.9 0.4 subtract_convert_fusion
  17.4 2.3 multiply_reduce_fusion
  19.7 15.9 %fusion.14 = (f32[128,16]{1,0:T(8,128)S(1)}, f32[128,16,256]{2,1,0:T(8,128)S(1)}) fusion(pred[128,256]{1,0:T(8,128)(4,1)S(1)} %iota_compare_fusion.12, bf16[128,256,576]{1,2,0:T(8,128)(2,1)} %param.17, bf16[128,16,576]{2,0,1:T(8,128)(2,1)} %get-tuple-element.3), kind=kOutput, calls=%fused_computation.28 | convolution fusion | flops 605550592 | bytes 42246144 | tf_op jit(solution)/shard_map/bhc,blc->bhl/dot_general | solution.py:67
  35.6 0.1 copy.73
  35.8 1.1 fusion.15
  37.0 0.1 copy.75
  37.1 0.1 copy.76
  37.2 16.0 %add_convert_fusion = bf16[128,16,512]{2,1,0:T(8,128)(2,1)} fusion(f32[128,512]{1,0:T(8,128)S(1)} %copy-done.6, f32[128,16]{1,0:T(8,128)S(1)} %copy.76, bf16[128,256,576]{1,2,0:T(8,128)(2,1)} %param.17, f32[128,16,256]{2,1,0:T(8,128)S(1)} %get-tuple-element.18, f32[128,16]{1,0:T(8,128)S(1)} %copy.75, f32[128,16]{1,0:T(8,128)S(1)} %copy.73, ...), kind=kOutput, calls=%fused_computation.6 | convolution fusion | flops 542638080 | bytes 38068224 | tf_op jit(solution)/shard_map/bhl,blc->bhc/dot_general | solution.py:77
  53.2 5.0 %fusion.16 = bf16[16,128,128]{1,2,0:T(8,128)(2,1)S(1)} fusion(bf16[16,512,128]{2,1,0:T(8,128)(2,1)} %param.24, bf16[128,16,512]{2,1,0:T(8,128)(2,1)} %add_convert_fusion), kind=kOutput, calls=%fused_computation.34 | convolution fusion | flops 268697600 | bytes 4718592 | tf_op jit(solution)/shard_map/bhc,hcv->bhv/dot_general | solution.py:79
  58.2 4.7 %multiply_reduce_fusion.1 = (f32[128]{0:T(128)S(1)}, f32[128,2048]{1,0:T(8,128)S(1)}) fusion(bf16[128,2048]{0,1:T(8,128)(2,1)S(1)} %bitcast.67, bf16[2048,2048]{1,0:T(8,128)(2,1)} %param.25, bf16[128,2048]{1,0:T(8,128)(2,1)S(1)} %copy-done.3), kind=kOutput, calls=%fused_computation.40 | convolution fusion | flops 1075314560 | bytes 10486272 | tf_op jit(solution)/shard_map/dot_general | solution.py:80
  63.0 0.1 copy.80
  63.1 0.1 eq.40
  63.2 0.4 fusion.20
  63.6 0.1 convert_element_type.143
  63.8 0.6 copy-done.7
  64.4 1.6 convolution_convert_fusion.3
  66.0 0.6 copy.84
  66.6 1.9 convolution_convert_fusion
  68.4 75.0 %all_to_all.21 = bf16[4,384,2048]{2,1,0:T(8,128)(2,1)S(1)} all-to-all(bf16[4,384,2048]{2,1,0:T(8,128)(2,1)S(1)} %bitcast.60), channel_id=1, replica_groups=mesh['rep'=2,'ep'=4] {'ep'}, dimensions={0} | all-to-all | bytes 12582912 | tf_op jit(solution)/shard_map/all_to_all | solution.py:102
  143.5 3.2 copy.85
  146.6 36.7 %fusion.53 = f32[16,96,1408]{2,1,0:T(8,128)} fusion(bf16[16,96,2048]{2,1,0:T(8,128)(2,1)} %bitcast.58, bf16[16,2048,1408]{2,1,0:T(8,128)(2,1)} %param.29), kind=kOutput, calls=%fused_computation.92 | convolution fusion | flops 8858370048 | bytes 107216896 | tf_op jit(solution)/shard_map/erh,ehi->eri/dot_general | solution.py:104
  183.3 64.8 %convolution_convert_fusion.1 = bf16[16,96,2048]{2,1,0:T(8,128)(2,1)} fusion(bf16[16,1408,2048]{2,1,0:T(8,128)(2,1)} %param.31, f32[16,96,1408]{2,1,0:T(8,128)} %fusion.53, bf16[16,96,2048]{2,1,0:T(8,128)(2,1)} %bitcast.59, bf16[16,2048,1408]{2,1,0:T(8,128)(2,1)} %param.30), kind=kOutput, calls=%fused_computation.5 | convolution fusion | flops 17732861952 | bytes 205783040 | tf_op jit(solution)/shard_map/eri,eih->erh/dot_general | solution.py:107
  248.1 6.6 %copy.86 = bf16[16,4,24,2048]{3,2,0,1:T(8,128)(2,1)} copy(bf16[16,4,24,2048]{3,2,1,0:T(8,128)(2,1)} %bitcast.61) | data formatting | bytes 12582912 | tf_op jit(solution)/shard_map/reshape | solution.py:108
  254.6 5.6 %all-to-all-start.1 = ((bf16[4,384,2048]{2,1,0:T(8,128)(2,1)}), bf16[4,384,2048]{2,1,0:T(8,128)(2,1)}, u32[]{:S(2)}, u32[]{:S(2)}) async-start(bf16[4,384,2048]{2,1,0:T(8,128)(2,1)} %bitcast.62), calls=%async_computation.1 | async-start | bytes 12582912 | tf_op jit(solution)/shard_map/all_to_all | solution.py:109
  260.3 0.2 copy.81
  260.5 0.2 fusion.30
  260.7 3.1 convert_bitcast_fusion
  263.8 2.7 copy.83
  266.4 7.3 %fusion.52 = f32[128,2816]{1,0:T(8,128)} fusion(bf16[2048,2816]{1,0:T(8,128)(2,1)} %param.26, f32[128,2048]{1,0:T(8,128)S(1)} %get-tuple-element.20, f32[128]{0:T(128)S(1)} %add_rsqrt_fusion), kind=kOutput, calls=%fused_computation.91 | convolution fusion | flops 1476919296 | bytes 14025216 | tf_op jit(solution)/shard_map/dot_general | solution.py:28
  273.7 56.7 %all-to-all-done.1 = bf16[4,384,2048]{2,1,0:T(8,128)(2,1)} async-done(((bf16[4,384,2048]{2,1,0:T(8,128)(2,1)}), bf16[4,384,2048]{2,1,0:T(8,128)(2,1)}, u32[]{:S(2)}, u32[]{:S(2)}) %all-to-all-start.1) | async-done | bytes 6291488 | tf_op jit(solution)/shard_map/all_to_all | solution.py:109
  330.4 6.5 %convolution_reduce_fusion = f32[128,2048]{1,0:T(8,128)} fusion(bf16[3,128,1536]{1,2,0:T(8,128)(2,1)S(1)} %bitcast.68, bf16[1536,2048,1]{1,0,2:T(8,128)(2,1)} %bitcast.22), kind=kOutput, calls=%fused_computation.29 | convolution fusion | flops 2416443392 | bytes 8519680 | tf_op jit(solution)/shard_map/dot_general | solution.py:110
  336.9 12.7 %fusion.8 = bf16[128,2048]{1,0:T(8,128)(2,1)} fusion(f32[128,2048]{1,0:T(8,128)} %convolution_reduce_fusion, f32[128,2048]{1,0:T(8,128)S(1)} %get-tuple-element.20, bf16[2816,2048]{1,0:T(8,128)(2,1)} %param.28, bf16[2048,2816]{1,0:T(8,128)(2,1)} %param.27, f32[128,2816]{1,0:T(8,128)} %fusion.52, f32[128]{0:T(128)S(1)} %add_rsqrt_fusion), kind=kOutput, calls=%fused_computation.18 | convolution fusion | flops 2956263424 | bytes 27132416 | tf_op jit(solution)/shard_map/dot_general | solution.py:30
  (32 shorter events, 0.3 us)
Async XLA Ops:
  0.6 2.9 copy-start
  0.6 6.6 %copy-start.2 = (bf16[128,2048]{1,0:T(8,128)(2,1)S(1)}, bf16[128,2048]{1,0:T(8,128)(2,1)}, u32[]{:S(2)}) copy-start(bf16[128,2048]{1,0:T(8,128)(2,1)} %param.16) | copy-start | bytes 1572868
  6.5 0.7 copy-start.5
  19.7 17.5 %copy-start.6 = (f32[128,512]{1,0:T(8,128)S(1)}, f32[128,512]{1,0:T(8,128)}, u32[]{:S(2)}) copy-start(f32[128,512]{1,0:T(8,128)} %copy.77) | copy-start | bytes 786436
  53.2 5.0 %copy-start.3 = (bf16[128,2048]{1,0:T(8,128)(2,1)S(1)}, bf16[128,2048]{1,0:T(8,128)(2,1)}, u32[]{:S(2)}) copy-start(bf16[128,2048]{1,0:T(8,128)(2,1)} %param.16) | copy-start | bytes 1572868
  58.2 4.8 %copy-start.8 = (s32[128,6]{0,1:T(8,128)S(1)}, s32[128,6]{0,1:T(8,128)}, u32[]{:S(2)}) copy-start(s32[128,6]{0,1:T(8,128)} %param.19) | copy-start | bytes 9220
  63.7 0.6 copy-start.7
  254.6 5.6 %copy-start.9 = (f32[128,6]{0,1:T(8,128)S(1)}, f32[128,6]{0,1:T(8,128)}, u32[]{:S(2)}) copy-start(f32[128,6]{0,1:T(8,128)} %param.20) | copy-start | bytes 9220
  254.6 75.7 %all-to-all-start.1 = ((bf16[4,384,2048]{2,1,0:T(8,128)(2,1)}), bf16[4,384,2048]{2,1,0:T(8,128)(2,1)}, u32[]{:S(2)}, u32[]{:S(2)}) async-start(bf16[4,384,2048]{2,1,0:T(8,128)(2,1)} %bitcast.62), calls=%async_computation.1 | async-start | bytes 12582912 | tf_op jit(solution)/shard_map/all_to_all | solution.py:109
  266.4 63.9 %copy-start.4 = (bf16[3,128,64,24]{1,3,2,0:T(8,128)(2,1)S(1)}, bf16[3,128,64,24]{1,3,2,0:T(8,128)(2,1)}, u32[]{:S(2)}) copy-start(bf16[3,128,64,24]{1,3,2,0:T(8,128)(2,1)} %copy.83) | copy-start | bytes 3538948
  336.8 12.7 %copy-start.1 = (bf16[2048,576]{0,1:T(8,128)(2,1)S(1)}, bf16[2048,576]{0,1:T(8,128)(2,1)}, u32[]{:S(2)}) copy-start(bf16[2048,576]{0,1:T(8,128)(2,1)} %param.22) | copy-start | bytes 7077892
where the time goes:
time: 350 us
  matrix products  187 us (53%)
  blocking collectives  75 us (21%)
  waiting for transfers between devices  56.7 us (16%)
  local copies, waits for them, and re-layouts  16.8 us (5%)
  other arithmetic  7.34 us (2%)
  starting transfers between devices  5.63 us (2%)
    all_to_all x1, blocking collectives, local(): recv = lax.all_to_all(send, 'ep', 0, 0, tiled=True)  75 us
    dot_general x1, matrix products, local(): jnp.einsum('eri,eih->erh', act, e_down, preferred_element_type=jnp.float32)  64.8 us
    all_to_all x1, waiting for transfers between devices, local(): ret = lax.all_to_all(back, 'ep', 0, 0, tiled=True)  56.7 us
    dot_general x1, matrix products, local(): jnp.einsum('erh,ehi->eri', xr, e_gate, preferred_element_type=jnp.float32)  36.7 us
    dot_general x1, matrix products, attention(): jnp.einsum('bhl,blc->bhc', p, cache, preferred_element_type=jnp.float32)  16 us
    dot_general x1, matrix products, attention(): jnp.einsum('bhc,blc->bhl', qf, cache, preferred_element_type=jnp.float32)  15.9 us
    dot_general x1, matrix products, swiglu(): jnp.dot((jax.nn.silu(g) * v).astype(jnp.bfloat16), wd, preferred_element_...  12.7 us
    dot_general x1, matrix products, swiglu(): g = jnp.dot(u, wg, preferred_element_type=jnp.float32)  7.27 us
  transfers between devices with their start and end apart: 1, of which 1 were waited for; matrix products, arithmetic and copies ran while one was open for 4% of the time, Pallas kernels for 0%

commit v1 on v0

v1 whole, which is shorter than its diff:
```python
import functools

import jax
import jax.numpy as jnp
from jax import lax
from jax.experimental import pallas as pl
from jax.experimental.pallas import tpu as pltpu
from jax.sharding import PartitionSpec as P

EPS = 1e-6
ROPE_BASE = 1.0e4
CAP = 32
COLS = 512
DOWN_SLOTS = 3


def rms(v):
    v = v.astype(jnp.float32)
    return v * lax.rsqrt(jnp.mean(v * v, axis=-1, keepdims=True) + EPS)


def rope(v, pos):
    half = v.shape[-1] // 2
    inv = ROPE_BASE ** (-2.0 * jnp.arange(half, dtype=jnp.float32) / v.shape[-1])
    ang = pos.astype(jnp.float32)[..., None] * inv
    cs = jnp.cos(ang)
    sn = jnp.sin(ang)
    v1 = v[..., :half]
    v2 = v[..., half:]
    return jnp.concatenate([v1 * cs - v2 * sn, v2 * cs + v1 * sn], axis=-1)


def attention(x, cache, lens, w_q, w_dkv, w_uk, w_uv, w_o):
    bsz = x.shape[0]
    heads, nope, kvl = w_uk.shape
    kvd = cache.shape[2]
    vh = w_uv.shape[2]
    qkd = nope + kvd - kvl
    xn = rms(x).astype(jnp.bfloat16)
    q = jnp.dot(xn, w_q, preferred_element_type=jnp.float32).astype(jnp.bfloat16).reshape(bsz, heads, qkd)
    kv = jnp.dot(xn, w_dkv, preferred_element_type=jnp.float32)
    kv_new = jnp.concatenate([rms(kv[:, :kvl]), rope(kv[:, kvl:], lens)], axis=-1).astype(jnp.bfloat16)
    q_lat = jnp.einsum('bhd,hdc->bhc', q[:, :, :nope], w_uk, preferred_element_type=jnp.float32).astype(jnp.bfloat16)
    q_rot = rope(q[:, :, nope:].astype(jnp.float32), lens[:, None]).astype(jnp.bfloat16)
    qf = jnp.concatenate([q_lat, q_rot], axis=-1)
    scale = qkd ** -0.5
    s = jnp.einsum('bhc,blc->bhl', qf, cache, preferred_element_type=jnp.float32) * scale
    live = jnp.arange(cache.shape[1])[None, None, :] < lens[:, None, None]
    s = jnp.where(live, s, -jnp.inf)
    s_new = jnp.einsum('bhc,bc->bh', qf, kv_new, preferred_element_type=jnp.float32) * scale
    mx = jnp.maximum(jnp.max(s, axis=2), s_new)
    e = jnp.exp(s - mx[:, :, None])
    e_new = jnp.exp(s_new - mx)
    den = jnp.sum(e, axis=2) + e_new
    p = (e / den[:, :, None]).astype(jnp.bfloat16)
    p_new = (e_new / den).astype(jnp.bfloat16)
    o_all = jnp.einsum('bhl,blc->bhc', p, cache, preferred_element_type=jnp.float32)
    o_lat = (o_all[:, :, :kvl] + p_new.astype(jnp.float32)[:, :, None] * kv_new[:, None, :kvl].astype(jnp.float32)).astype(jnp.bfloat16)
    o = jnp.einsum('bhc,hcv->bhv', o_lat, w_uv, preferred_element_type=jnp.float32).astype(jnp.bfloat16).reshape(bsz, heads * vh)
    a = jnp.dot(o, w_o, preferred_element_type=jnp.float32)
    return (x.astype(jnp.float32) + a).astype(jnp.bfloat16), kv_new


def dot(a, b):
    return jnp.dot(a, b, preferred_element_type=jnp.float32)


def moe_kernel(u_ref, h1_ref, meta_ref, sg, su, sd, eg, eu, ed, y_ref,
               gbuf, ubuf, dbuf, xall, act, sact, gate, outc, comb, uall, mall, s1, r1, s2, r2, own, shf,
               gsem, usem, dsem, us_send, us_recv, ms_send, ms_recv, s1_send, s1_recv, s2_send, s2_recv):
    n_loc = eg.shape[0]
    bsz, hid = u_ref.shape
    inter = eg.shape[2]
    n_col = hid // COLS
    pairs = n_loc // 2
    n_down = n_col * pairs
    half = bsz // 2
    me = lax.axis_index('ep')
    partner = {'ep': me + 1 - 2 * lax.rem(me, 2)}
    across = {'ep': lax.rem(me + 2, 4)}

    def gate_copy(e, slot):
        return pltpu.make_async_copy(eg.at[e], gbuf.at[slot], gsem.at[slot])

    def up_copy(e, slot):
        return pltpu.make_async_copy(eu.at[e], ubuf.at[slot], usem.at[slot])

    def sgate_copy(i):
        return pltpu.make_async_copy(sg.at[:, pl.ds(i * inter, inter)], gbuf.at[i], gsem.at[i])

    def sup_copy(i):
        return pltpu.make_async_copy(su.at[:, pl.ds(i * inter, inter)], ubuf.at[i], usem.at[i])

    def down_copy(j, slot):
        c = j // pairs
        e = lax.rem(j, pairs)
        return pltpu.make_async_copy(
            ed.at[pl.ds(2 * e, 2), :, pl.ds(pl.multiple_of(c * COLS, COLS), COLS)], dbuf.at[slot], dsem.at[slot])

    def sdown_copy(c, slot):
        return pltpu.make_async_copy(sd.at[:, :, pl.ds(c * COLS, COLS)], dbuf.at[slot], dsem.at[slot])

    def remote(src, dst, send, recv, dev):
        return pltpu.make_async_remote_copy(src_ref=src, dst_ref=dst, send_sem=send, recv_sem=recv,
                                            device_id=dev, device_id_type=pl.DeviceIdType.MESH)

    for i in range(2):
        sgate_copy(i).start()
        sup_copy(i).start()

    barrier = pltpu.get_barrier_semaphore()
    for dev in (partner, across):
        pl.semaphore_signal(barrier, inc=1, device_id=dev, device_id_type=pl.DeviceIdType.MESH)
    pl.semaphore_wait(barrier, 2)

    m_across = remote(meta_ref, mall.at[1], ms_send.at[1], ms_recv.at[1], across)
    u_across = [remote(u_ref.at[pl.ds(i * half, half)], uall.at[1, pl.ds(i * half, half)],
                       us_send.at[1 + i], us_recv.at[1 + i], across) for i in range(2)]
    m_partner = remote(meta_ref, mall.at[0], ms_send.at[0], ms_recv.at[0], partner)
    u_partner = remote(u_ref, uall.at[0], us_send.at[0], us_recv.at[0], partner)
    m_relay = remote(mall.at[1], mall.at[2], ms_send.at[2], ms_recv.at[2], partner)
    u_relay = [remote(uall.at[1, pl.ds(i * half, half)], uall.at[2, pl.ds(i * half, half)],
                      us_send.at[3 + i], us_recv.at[3 + i], partner) for i in range(2)]
    m_across.start()
    u_across[0].start()
    u_across[1].start()
    m_partner.start()
    u_partner.start()

    def glu(lhs, e, slot, dst, g_wait, u_wait, g_next, u_next):
        g_wait.wait()
        gate[...] = dot(lhs, gbuf[slot])
        g_next()
        u_wait.wait()
        v = dot(lhs, ubuf[slot])
        dst[...] = (jax.nn.silu(gate[...]) * v).astype(jnp.bfloat16)
        u_next()

    for i in range(2):
        glu(u_ref[...], i, i, sact.at[i], sgate_copy(i), sup_copy(i),
            lambda: gate_copy(i, i).start(), lambda: up_copy(i, i).start())

    for j in range(DOWN_SLOTS):
        down_copy(j, j).start()

    def dispatch(q, m, u):
        first = (me * n_loc).astype(jnp.float32)
        mine = lax.broadcasted_iota(jnp.int32, (n_loc, bsz), 0).astype(jnp.float32) + first
        hit = jnp.zeros((n_loc, bsz), jnp.float32)
        wgt = jnp.zeros((n_loc, bsz), jnp.float32)
        for k in range(6):
            eq = m[k:k + 1, :] == mine
            hit = jnp.where(eq, 1.0, hit)
            wgt = jnp.where(eq, m[8 + k:9 + k, :], wgt)
        row = lax.broadcasted_iota(jnp.int32, (bsz, bsz), 0)
        col = lax.broadcasted_iota(jnp.int32, (bsz, bsz), 1)
        low = jnp.where(row < col, 1.0, 0.0).astype(jnp.bfloat16)
        rank = jnp.where(hit > 0.0, dot(hit.astype(jnp.bfloat16), low), -1.0)
        slot = lax.broadcasted_iota(jnp.int32, (CAP, bsz), 0).astype(jnp.float32)
        sel = []
        ct = []
        for e in range(n_loc):
            at = slot == rank[e:e + 1, :]
            sel.append(jnp.where(at, 1.0, 0.0).astype(jnp.bfloat16))
            ct.append(jnp.where(at, wgt[e:e + 1, :], 0.0))
        c0 = jnp.concatenate(ct, axis=0).T
        for i in range(3):
            ci = c0.astype(jnp.bfloat16)
            comb[q, pl.ds(i * bsz, bsz), :] = ci
            c0 = c0 - ci.astype(jnp.float32)
        xall[q] = dot(jnp.concatenate(sel, axis=0), u).astype(jnp.bfloat16)

    dispatch(0, meta_ref[...], u_ref[...])
    m_partner.wait_recv()
    u_partner.wait_recv()
    dispatch(1, mall[0], uall[0])
    m_across.wait_recv()
    m_relay.start()
    for i in range(2):
        u_across[i].wait_recv()
        u_relay[i].start()
    dispatch(2, mall[1], uall[1])
    m_relay.wait_recv()
    for i in range(2):
        u_relay[i].wait_recv()
    dispatch(3, mall[2], uall[2])

    def expert(e, _):
        slot = lax.rem(e, 2)
        lhs = xall[:, pl.ds(pl.multiple_of(e * CAP, CAP), CAP), :].reshape(4 * CAP, hid)

        def g_next():
            @pl.when(e < n_loc - 2)
            def _():
                gate_copy(e + 2, slot).start()

        def u_next():
            @pl.when(e < n_loc - 2)
            def _():
                up_copy(e + 2, slot).start()

        glu(lhs, e, slot, act.at[e], gate_copy(e, slot), up_copy(e, slot), g_next, u_next)
        return 0

    lax.fori_loop(0, n_loc, expert, 0)

    def ring1(c):
        return remote(s1.at[c], r1.at[c], s1_send.at[c], s1_recv.at[c], partner)

    def ring2(c):
        return remote(s2.at[c], r2.at[c], s2_send.at[c], s2_recv.at[c], across)

    def fold(c):
        ring1(c).wait_recv()
        s2[c] = s2[c] + r1[c, 1]
        own[c] = own[c] + r1[c, 0]

    def down_step(j, c, e):
        slot = lax.rem(j, DOWN_SLOTS)
        down_copy(j, slot).wait()
        for i in range(2):
            res = dot(act[2 * e + i], dbuf[slot, i]).astype(jnp.bfloat16)
            outc[:, pl.ds(pl.multiple_of((2 * e + i) * CAP, CAP), CAP), :] = res.reshape(4, CAP, COLS)

        @pl.when(j + DOWN_SLOTS < n_down)
        def _():
            down_copy(j + DOWN_SLOTS, slot).start()

    def combine(q):
        p = dot(comb[q], outc[q])
        return p[:bsz] + p[bsz:2 * bsz] + p[2 * bsz:]

    def column(c, _):
        def step(e, _):
            down_step(c * pairs + e, c, e)

            @pl.when((c > 0) & (e == 2))
            def _():
                fold(c - 1)

            @pl.when((c > 0) & (e == 3))
            def _():
                ring2(c - 1).start()
            return 0

        lax.fori_loop(0, pairs, step, 0)
        s1[c, 1] = combine(3)
        s1[c, 0] = combine(1)
        s2[c] = combine(2)
        own[c] = combine(0)
        ring1(c).start()
        return 0

    lax.fori_loop(0, n_col, column, 0)

    for c in range(min(DOWN_SLOTS, n_col)):
        sdown_copy(c, (n_down + c) % DOWN_SLOTS).start()
    for c in range(n_col):
        slot = (n_down + c) % DOWN_SLOTS
        sdown_copy(c, slot).wait()
        shf[c] = dot(sact[0], dbuf[slot, 0]) + dot(sact[1], dbuf[slot, 1])
        if c + DOWN_SLOTS < n_col:
            sdown_copy(c + DOWN_SLOTS, slot).start()
        if c == 0:
            fold(n_col - 1)
        if c == 1:
            ring2(n_col - 1).start()

    for c in range(n_col):
        ring2(c).wait_recv()
        cols = pl.ds(c * COLS, COLS)
        y = h1_ref[:, cols].astype(jnp.float32) + shf[c] + (own[c] + r2[c])
        y_ref[:, cols] = y.astype(jnp.bfloat16)

    for copy in (m_across, *u_across, m_partner, u_partner, m_relay, *u_relay):
        copy.wait_send()
    for c in range(n_col):
        ring1(c).wait_send()
        ring2(c).wait_send()


def moe(u, h1, meta, s_gate, s_up, s_down, e_gate, e_up, e_down):
    bsz, hid = u.shape
    n_loc, _, inter = e_gate.shape
    n_col = hid // COLS
    bf16, f32 = jnp.bfloat16, jnp.float32
    vm = pl.BlockSpec(memory_space=pltpu.VMEM)
    hbm = pl.BlockSpec(memory_space=pl.ANY)
    dma = pltpu.SemaphoreType.DMA
    return pl.pallas_call(
        moe_kernel,
        out_shape=jax.ShapeDtypeStruct((bsz, hid), bf16),
        in_specs=[vm] * 3 + [hbm] * 6,
        out_specs=vm,
        scratch_shapes=[
            pltpu.VMEM((2, hid, inter), bf16),
            pltpu.VMEM((2, hid, inter), bf16),
            pltpu.VMEM((DOWN_SLOTS, 2, inter, COLS), bf16),
            pltpu.VMEM((4, n_loc * CAP, hid), bf16),
            pltpu.VMEM((n_loc, 4 * CAP, inter), bf16),
            pltpu.VMEM((2, bsz, inter), bf16),
            pltpu.VMEM((bsz, inter), f32),
            pltpu.VMEM((4, n_loc * CAP, COLS), bf16),
            pltpu.VMEM((4, 3 * bsz, n_loc * CAP), bf16),
            pltpu.VMEM((3, bsz, hid), bf16),
            pltpu.VMEM((3, 16, bsz), f32),
            pltpu.VMEM((n_col, 2, bsz, COLS), f32),
            pltpu.VMEM((n_col, 2, bsz, COLS), f32),
            pltpu.VMEM((n_col, bsz, COLS), f32),
            pltpu.VMEM((n_col, bsz, COLS), f32),
            pltpu.VMEM((n_col, bsz, COLS), f32),
            pltpu.VMEM((n_col, bsz, COLS), f32),
            dma((2,)), dma((2,)), dma((DOWN_SLOTS,)),
            dma((5,)), dma((5,)), dma((3,)), dma((3,)),
            dma((n_col,)), dma((n_col,)), dma((n_col,)), dma((n_col,)),
        ],
        compiler_params=pltpu.CompilerParams(
            collective_id=0, has_side_effects=True, vmem_limit_bytes=67043328),
        name='moe',
    )(u, h1, meta, s_gate, s_up, s_down.reshape(2, inter, hid), e_gate, e_up, e_down)


def solution(mesh):
    tok_spec = P(('rep', 'ep'))
    row_spec = P(('rep', 'ep'), None)
    cache_spec = P(('rep', 'ep'), None, None)
    exp_spec = P('ep', None, None)

    def local(x, cache, lens, ids, rw, w_q, w_dkv, w_uk, w_uv, w_o, s_gate, s_up, s_down, e_gate, e_up, e_down):
        h1, kv_new = attention(x, cache, lens, w_q, w_dkv, w_uk, w_uv, w_o)
        u = rms(h1).astype(jnp.bfloat16)
        meta = jnp.concatenate([jnp.pad(ids.astype(jnp.float32), ((0, 0), (0, 2))), jnp.pad(rw, ((0, 0), (0, 2)))], axis=1).T
        y = moe(u, h1, meta, s_gate, s_up, s_down, e_gate, e_up, e_down)
        return y, kv_new

    in_specs = (row_spec, cache_spec, tok_spec, row_spec, row_spec) + (P(),) * 8 + (exp_spec,) * 3
    return jax.shard_map(local, mesh=mesh, in_specs=in_specs, out_specs=(row_spec, row_spec), check_vma=False)
```

time: 350 us -> 178 us (0.51)
  matrix products: 187 us -> 52.5 us
  Pallas kernels: 0 us -> 111 us
  blocking collectives: 75 us -> 0 us
  waiting for transfers between devices: 56.7 us -> 0 us
  local copies, waits for them, and re-layouts: 16.8 us -> 6.13 us
  starting transfers between devices: 5.63 us -> 0 us
    dot_general x9 -> x0, matrix products: 135 us -> none  [the longest x1 64.8 us: local(): jnp.einsum('eri,eih->erh', act, e_down, preferred_element_type=jnp.float32)]
    pallas_call x0 -> x1, Pallas kernels: none -> 111 us  [moe(): pl.pallas_call(moe_kernel, out_shape=jax.ShapeDtypeStruct((bsz, hid), bf1...]
    all_to_all x1 -> x0, blocking collectives: 75 us -> none  [local(): recv = lax.all_to_all(send, 'ep', 0, 0, tiled=True)]
    all_to_all x1 -> x0, waiting for transfers between devices: 56.7 us -> none  [local(): ret = lax.all_to_all(back, 'ep', 0, 0, tiled=True)]
    reshape x2 -> x0, local copies, waits for them, and re-layouts: 9.72 us -> none  [the longest x1 6.56 us: local(): out.reshape(e_loc, n, cape, hid).transpose(1, 0, 2, 3)]
    all_to_all x1 -> x0, starting transfers between devices: 5.63 us -> none  [local(): ret = lax.all_to_all(back, 'ep', 0, 0, tiled=True)]
  transfers between devices with their start and end apart: 1 -> 0, of which waited for: 1 -> 0; matrix products, arithmetic and copies ran while one was open for 4% -> 0% of each run, Pallas kernels for 0% -> 0%
where the time goes in v1:
time: 178 us
  Pallas kernels  111 us (62%)
  matrix products  52.5 us (29%)
  other arithmetic  7.2 us (4%)
  local copies, waits for them, and re-layouts  6.13 us (3%)
    pallas_call x1, Pallas kernels, moe(): pl.pallas_call(moe_kernel, out_shape=jax.ShapeDtypeStruct((bsz, hid), bf1...  111 us
    dot_general x1, matrix products, attention(): jnp.einsum('bhc,blc->bhl', qf, cache, preferred_element_type=jnp.float32)  16.9 us
    dot_general x1, matrix products, attention(): jnp.einsum('bhl,blc->bhc', p, cache, preferred_element_type=jnp.float32)  16 us
    dot_general x1, matrix products, attention(): jnp.dot(xn, w_q, preferred_element_type=jnp.float32).astype(jnp.bfloat16)  6.49 us
    unnamed x23, local copies, waits for them, and re-layouts  5.03 us
    dot_general x1, matrix products, attention(): jnp.einsum('bhc,hcv->bhv', o_lat, w_uv, preferred_element_type=jnp.float32)  4.9 us
    dot_general x1, matrix products, attention(): a = jnp.dot(o, w_o, preferred_element_type=jnp.float32)  4.77 us

profile of v1, /device:TPU:0, one launch (start us, length us, event | category | flops | bytes accessed | tf_op | source)
XLA Modules:
  0.0 177.7 jit_solution(14603127483888256299)
XLA Ops:
  0.6 0.0 copy-start.9
  0.6 1.2 fusion.16
  1.9 0.0 copy-start
  1.9 2.7 %fusion.24 = f32[128,576]{0,1:T(8,128)S(1)} fusion(bf16[2048,576]{0,1:T(8,128)(2,1)} %param.22, bf16[128,2048]{1,0:T(8,128)(2,1)} %param.16, f32[128]{0:T(128)S(1)} %add_rsqrt_fusion.2), kind=kOutput, calls=%fused_computation.37 | convolution fusion | flops 302776320 | bytes 3179008 | tf_op jit(solution)/shard_map/dot_general | solution.py:41
  4.6 0.1 multiply_reduce_fusion.1
  4.8 0.0 copy-done.9
  4.8 0.0 copy-start.4
  4.8 0.1 multiply_cosine_fusion
  5.0 0.5 copy-done.4
  5.4 0.0 copy-start.6
  5.4 0.1 copy.68
  5.6 0.1 copy.50
  5.7 0.4 copy-done.6
  6.1 0.1 copy.51
  6.2 0.0 copy-done
  6.2 6.5 %convolution_convert_fusion = bf16[128,3072]{1,0:T(8,128)(2,1)S(1)} fusion(bf16[2048,3072]{1,0:T(8,128)(2,1)} %param.21, bf16[128,2048]{1,0:T(8,128)(2,1)S(1)} %copy-done, f32[128]{0:T(128)S(1)} %add_rsqrt_fusion.2), kind=kOutput, calls=%fused_computation.4 | convolution fusion | flops 1611792384 | bytes 13894144 | tf_op jit(solution)/shard_map/dot_general | solution.py:40
  12.7 0.4 copy.47
  13.1 0.3 copy.67
  13.4 0.0 copy-start.3
  13.4 0.1 convert_element_type.68
  13.5 0.5 subtract_convert_fusion
  14.0 1.0 copy-done.3
  15.0 0.8 convert_bitcast_fusion
  15.7 0.9 multiply_reduce_fusion
  16.6 0.1 iota_compare_fusion
  16.7 16.9 %fusion.9 = (f32[128,16]{1,0:T(8,128)S(1)}, f32[128,16,256]{2,1,0:T(8,128)}) fusion(pred[128,256]{1,0:T(8,128)(4,1)S(1)} %iota_compare_fusion, bf16[128,256,576]{1,2,0:T(8,128)(2,1)} %param.17, bf16[128,16,576]{2,0,1:T(8,128)(2,1)S(1)} %get-tuple-element.3), kind=kOutput, calls=%fused_computation.16 | convolution fusion | flops 605550592 | bytes 42246144 | tf_op jit(solution)/shard_map/bhc,blc->bhl/dot_general | solution.py:47
  33.6 0.0 copy-start.5
  33.6 0.1 copy.54
  33.8 2.6 %fusion.10 = f32[128,16]{1,0:T(8,128)S(1)} fusion(f32[128,16,256]{2,1,0:T(8,128)} %get-tuple-element.15, f32[128,16]{1,0:T(8,128)S(1)} %copy.54, pred[128,256]{1,0:T(8,128)(4,1)S(1)} %iota_compare_fusion), kind=kLoop, calls=%fused_computation.17 | loop fusion | flops 2095104 | bytes 2146304 | tf_op jit(solution)/shard_map/reduce_sum | solution.py:54
  36.3 0.1 copy.55
  36.4 0.1 copy.56
  36.5 0.1 copy.57
  36.6 0.0 copy-done.5
  36.6 0.1 copy.58
  36.8 0.0 copy-done.1
  36.8 16.0 %add_convert_fusion = bf16[128,16,512]{2,1,0:T(8,128)(2,1)} fusion(f32[128,512]{1,0:T(8,128)S(1)} %copy.58, f32[128,16]{1,0:T(8,128)S(1)} %copy.57, bf16[128,256,576]{1,2,0:T(8,128)(2,1)} %param.17, f32[128,16,256]{2,1,0:T(8,128)S(1)} %copy-done.1, f32[128,16]{1,0:T(8,128)S(1)} %copy.56, f32[128,16]{1,0:T(8,128)S(1)} %copy.54, ...), kind=kOutput, calls=%fused_computation.3 | convolution fusion | flops 542638080 | bytes 38068224 | tf_op jit(solution)/shard_map/bhl,blc->bhc/dot_general | solution.py:57
  52.8 4.9 %fusion.11 = bf16[16,128,128]{1,2,0:T(8,128)(2,1)S(1)} fusion(bf16[16,512,128]{2,1,0:T(8,128)(2,1)} %param.24, bf16[128,16,512]{2,1,0:T(8,128)(2,1)} %add_convert_fusion), kind=kOutput, calls=%fused_computation.22 | convolution fusion | flops 268697600 | bytes 4718592 | tf_op jit(solution)/shard_map/bhc,hcv->bhv/dot_general | solution.py:59
  57.7 0.0 copy-start.7
  57.7 0.0 copy-start.8
  57.7 4.8 %fusion.14 = (f32[128]{0:T(128)S(1)}, bf16[128,2048]{1,0:T(8,128)(2,1)S(1)}) fusion(bf16[128,2048]{0,1:T(8,128)(2,1)S(1)} %bitcast.21, bf16[2048,2048]{1,0:T(8,128)(2,1)} %param.25, bf16[128,2048]{1,0:T(8,128)(2,1)S(1)} %copy-done), kind=kOutput, calls=%fused_computation.23 | convolution fusion | flops 1075314560 | bytes 9961984 | tf_op jit(solution)/shard_map/dot_general | solution.py:60
  62.5 0.0 copy-start.2
  62.5 0.8 copy-done.2
  63.3 0.9 fusion.15.u_ref
  64.2 0.0 copy-done.7
  64.2 0.0 copy-done.8
  64.2 0.6 fusion.27.meta_ref
  64.8 111.0 %moe.1 = bf16[128,2048]{1,0:T(8,128)(2,1)} custom-call(bf16[128,2048]{1,0:T(8,128)(2,1)} %fusion.15.u_ref, bf16[128,2048]{1,0:T(8,128)(2,1)} %copy-done.2, f32[16,128]{1,0:T(8,128)} %fusion.27.meta_ref, bf16[2048,2816]{1,0:T(8,128)(2,1)} %sg.1, bf16[2048,2816]{1,0:T(8,128)(2,1)} %su.1, bf16[2,1408,2048]{2,1,0:T(8,128)(2,1)} %bitcast.18, ...), custom_call_target="tpu_custom_call" | custom-call | tf_op jit(solution)/shard_map/moe/pallas_call | solution.py:290
  175.9 1.9 %copy.78 = bf16[128,2048]{1,0:T(8,128)(2,1)} copy(bf16[128,2048]{1,0:T(8,128)(2,1)} %moe.1) | data formatting | bytes 1048576
  (13 shorter events, 0.2 us)
Async XLA Ops:
  0.6 4.1 %copy-start.9 = (s32[128]{0:T(128)S(1)}, s32[128]{0:T(128)}, u32[]{:S(2)}) copy-start(s32[128]{0:T(128)} %param.18) | copy-start | bytes 1540
  1.9 4.3 %copy-start = (bf16[128,2048]{1,0:T(8,128)(2,1)S(1)}, bf16[128,2048]{1,0:T(8,128)(2,1)}, u32[]{:S(2)}) copy-start(bf16[128,2048]{1,0:T(8,128)(2,1)} %param.16) | copy-start | bytes 1572868
  4.8 0.7 copy-start.4
  5.4 0.7 copy-start.6
  13.4 1.6 copy-start.3
  33.6 3.0 %copy-start.5 = (bf16[128,512]{0,1:T(8,128)(2,1)S(1)}, bf16[128,512]{0,1:T(8,128)(2,1)}, u32[]{:S(2)}) copy-start(bf16[128,512]{0,1:T(8,128)(2,1)} %copy-done.4) | copy-start | bytes 393220
  33.6 3.2 %copy-start.1 = (f32[128,16,256]{2,1,0:T(8,128)S(1)}, f32[128,16,256]{2,1,0:T(8,128)}, u32[]{:S(2)}) copy-start(f32[128,16,256]{2,1,0:T(8,128)} %get-tuple-element.15) | copy-start | bytes 6291460
  57.7 6.5 %copy-start.7 = (s32[128,6]{0,1:T(8,128)S(1)}, s32[128,6]{0,1:T(8,128)}, u32[]{:S(2)}) copy-start(s32[128,6]{0,1:T(8,128)} %param.19) | copy-start | bytes 9220
  57.7 6.5 %copy-start.8 = (f32[128,6]{0,1:T(8,128)S(1)}, f32[128,6]{0,1:T(8,128)}, u32[]{:S(2)}) copy-start(f32[128,6]{0,1:T(8,128)} %param.20) | copy-start | bytes 9220
  62.5 0.8 copy-start.2

commit v2 on v1

--- a/solution.py
+++ b/solution.py
@@ -1,5 +1,3 @@
-import functools
-
 import jax
 import jax.numpy as jnp
 from jax import lax
@@ -12,57 +10,184 @@
 CAP = 32
 COLS = 512
 DOWN_SLOTS = 3
-
-
-def rms(v):
-    v = v.astype(jnp.float32)
-    return v * lax.rsqrt(jnp.mean(v * v, axis=-1, keepdims=True) + EPS)
-
-
-def rope(v, pos):
-    half = v.shape[-1] // 2
-    inv = ROPE_BASE ** (-2.0 * jnp.arange(half, dtype=jnp.float32) / v.shape[-1])
-    ang = pos.astype(jnp.float32)[..., None] * inv
-    cs = jnp.cos(ang)
-    sn = jnp.sin(ang)
-    v1 = v[..., :half]
-    v2 = v[..., half:]
-    return jnp.concatenate([v1 * cs - v2 * sn, v2 * cs + v1 * sn], axis=-1)
-
-
-def attention(x, cache, lens, w_q, w_dkv, w_uk, w_uv, w_o):
-    bsz = x.shape[0]
-    heads, nope, kvl = w_uk.shape
-    kvd = cache.shape[2]
-    vh = w_uv.shape[2]
-    qkd = nope + kvd - kvl
-    xn = rms(x).astype(jnp.bfloat16)
-    q = jnp.dot(xn, w_q, preferred_element_type=jnp.float32).astype(jnp.bfloat16).reshape(bsz, heads, qkd)
-    kv = jnp.dot(xn, w_dkv, preferred_element_type=jnp.float32)
-    kv_new = jnp.concatenate([rms(kv[:, :kvl]), rope(kv[:, kvl:], lens)], axis=-1).astype(jnp.bfloat16)
-    q_lat = jnp.einsum('bhd,hdc->bhc', q[:, :, :nope], w_uk, preferred_element_type=jnp.float32).astype(jnp.bfloat16)
-    q_rot = rope(q[:, :, nope:].astype(jnp.float32), lens[:, None]).astype(jnp.bfloat16)
-    qf = jnp.concatenate([q_lat, q_rot], axis=-1)
-    scale = qkd ** -0.5
-    s = jnp.einsum('bhc,blc->bhl', qf, cache, preferred_element_type=jnp.float32) * scale
-    live = jnp.arange(cache.shape[1])[None, None, :] < lens[:, None, None]
-    s = jnp.where(live, s, -jnp.inf)
-    s_new = jnp.einsum('bhc,bc->bh', qf, kv_new, preferred_element_type=jnp.float32) * scale
-    mx = jnp.maximum(jnp.max(s, axis=2), s_new)
-    e = jnp.exp(s - mx[:, :, None])
-    e_new = jnp.exp(s_new - mx)
-    den = jnp.sum(e, axis=2) + e_new
-    p = (e / den[:, :, None]).astype(jnp.bfloat16)
-    p_new = (e_new / den).astype(jnp.bfloat16)
-    o_all = jnp.einsum('bhl,blc->bhc', p, cache, preferred_element_type=jnp.float32)
-    o_lat = (o_all[:, :, :kvl] + p_new.astype(jnp.float32)[:, :, None] * kv_new[:, None, :kvl].astype(jnp.float32)).astype(jnp.bfloat16)
-    o = jnp.einsum('bhc,hcv->bhv', o_lat, w_uv, preferred_element_type=jnp.float32).astype(jnp.bfloat16).reshape(bsz, heads * vh)
-    a = jnp.dot(o, w_o, preferred_element_type=jnp.float32)
-    return (x.astype(jnp.float32) + a).astype(jnp.bfloat16), kv_new
+GROUP = 8
+CACHE_SLOTS = 6
+Q_PARTS = 4
 
 
 def dot(a, b):
     return jnp.dot(a, b, preferred_element_type=jnp.float32)
+
+
+def attn_kernel(lens_ref, x_ref, tab_ref, cache, wq, wdkv, wuk, wuv, wo, h1_ref, u_ref, kv_ref,
+                cbuf, qbuf, dkvbuf, ukbuf, uvbuf, obuf, qf, kvr, sbuf, ol, oall,
+                csem, qsem, wsem):
+    bsz, hid = x_ref.shape
+    heads, nope, lat = wuk.shape
+    kvd, rows = cache.shape[1], cache.shape[2]
+    rot = kvd - lat
+    vh = wuv.shape[2]
+    qkd = nope + rot
+    steps = bsz // GROUP
+    part = heads * qkd // Q_PARTS
+    scale = qkd ** -0.5
+    f32, bf16 = jnp.float32, jnp.bfloat16
+
+    def c_copy(i, slot):
+        return pltpu.make_async_copy(cache.at[pl.ds(i * GROUP, GROUP)], cbuf.at[slot], csem.at[slot])
+
+    q_copies = [pltpu.make_async_copy(wq.at[:, pl.ds(i * part, part)], qbuf.at[i], qsem.at[i]) for i in range(Q_PARTS)]
+    dkv_copy = pltpu.make_async_copy(wdkv, dkvbuf, wsem.at[0])
+    uk_copy = pltpu.make_async_copy(wuk, ukbuf, wsem.at[1])
+    uv_copy = pltpu.make_async_copy(wuv, uvbuf, wsem.at[2])
+    o_copy = pltpu.make_async_copy(wo, obuf, wsem.at[3])
+    dkv_copy.start()
+    uk_copy.start()
+    for copy in q_copies:
+        copy.start()
+    for i in range(CACHE_SLOTS):
+        c_copy(i, i).start()
+    uv_copy.start()
+    o_copy.start()
+
+    x = x_ref[...].astype(f32)
+    xn = (x * lax.rsqrt(jnp.mean(x * x, axis=-1, keepdims=True) + EPS)).astype(bf16)
+    cos_t = tab_ref[:rot // 2]
+    sin_t = tab_ref[rot // 2:]
+    cos = jnp.concatenate([cos_t] * 4, axis=0).T
+    sin = jnp.concatenate([-sin_t, sin_t] * 2, axis=0).T
+
+    dkv_copy.wait()
+    kv = lax.dot_general(dkvbuf[...], xn, (((1,), (1,)), ((), ())), preferred_element_type=f32)
+    c = kv[:lat]
+    c = c * lax.rsqrt(jnp.mean(c * c, axis=0, keepdims=True) + EPS)
+    v1 = kv[lat:lat + rot // 2]
+    v2 = kv[lat + rot // 2:]
+    kv = jnp.concatenate([c, v1 * cos_t - v2 * sin_t, v2 * cos_t + v1 * sin_t], axis=0).astype(bf16)
+    kv_ref[...] = kv
+    kvr[...] = jnp.concatenate([kv.astype(f32), jnp.zeros((kvr.shape[1] - kvd, bsz), f32)], axis=0).T
+
+    uk_copy.wait()
+    lane = lax.broadcasted_iota(jnp.int32, (bsz, 2 * rot), 1)
+    for i in range(Q_PARTS):
+        q_copies[i].wait()
+        q = dot(xn, qbuf[i]).astype(bf16).astype(f32)
+        for j in range(part // (2 * qkd)):
+            at = 2 * qkd * j
+            h = i * (part // qkd) + 2 * j
+            mid = q[:, at + nope:at + 2 * nope]
+            last = q[:, at + 2 * nope:at + 3 * nope]
+            low = lane < rot
+            flip = pltpu.roll(mid, rot, 1)
+            n_a = q[:, at:at + nope]
+            n_b = jnp.where(low, flip, pltpu.roll(last, rot, 1))
+            r = jnp.where(low, mid, last)
+            swap = jnp.where(lax.rem(lane, rot) < rot // 2, pltpu.roll(r, 2 * rot - rot // 2, 1), pltpu.roll(r, rot // 2, 1))
+            r = (r * cos + swap * sin).astype(bf16).astype(f32)
+            for k, n, z in ((0, n_a, r), (1, n_b, pltpu.roll(r, rot, 1))):
+                to = pl.ds(h + k, bsz, stride=heads)
+                ql = dot(n.astype(bf16), ukbuf[h + k]).astype(bf16).astype(f32)
+                for t in range(lat // 128):
+                    qf[t, to, :] = ql[:, t * 128:(t + 1) * 128]
+                qf[lat // 128, to, :] = jnp.where(low, z, 0.0)
+
+    def query(b):
+        to = pl.ds(pl.multiple_of(b * heads, heads), heads)
+        return jnp.concatenate([qf[t, to, :] for t in range(qf.shape[0])], axis=1)
+
+    def scores(i, slot):
+        for g in range(GROUP):
+            qg = query(i * GROUP + g)
+            sbuf[pl.ds(g * heads, heads), :] = dot(qg[:, :kvd].astype(bf16), cbuf[slot, g])
+
+    def attend(i, slot):
+        col = lax.broadcasted_iota(jnp.int32, (heads, rows), 1)
+        for g in range(GROUP):
+            b = i * GROUP + g
+            to = pl.ds(pl.multiple_of(b * heads, heads), heads)
+            new = kvr[pl.ds(b, 1), :]
+            s_new = jnp.sum(query(b) * new, axis=1, keepdims=True) * scale
+            s = sbuf[pl.ds(g * heads, heads), :] * scale
+            s = jnp.where(col < lens_ref[b], s, -jnp.inf)
+            mx = jnp.maximum(jnp.max(s, axis=1, keepdims=True), s_new)
+            e = jnp.exp(s - mx)
+            e_new = jnp.exp(s_new - mx)
+            den = jnp.sum(e, axis=1, keepdims=True) + e_new
+            p = (e / den).astype(bf16)
+            p_new = (e_new / den).astype(bf16).astype(f32)
+            o = lax.dot_general(p, cbuf[slot, g, :lat, :], (((1,), (1,)), ((), ())), preferred_element_type=f32)
+            o = o + p_new * new[:, :lat]
+            for t in range(lat // 128):
+                ol[t, to, :] = o[:, t * 128:(t + 1) * 128]
+
+    c_copy(0, 0).wait()
+    scores(0, 0)
+
+    def step(i, _):
+        slot = lax.rem(i, CACHE_SLOTS)
+        attend(i, slot)
+
+        @pl.when(i + 1 < steps)
+        def _():
+            c_copy(i + 1, lax.rem(i + 1, CACHE_SLOTS)).wait()
+            scores(i + 1, lax.rem(i + 1, CACHE_SLOTS))
+
+        @pl.when(i + CACHE_SLOTS < steps)
+        def _():
+            c_copy(i + CACHE_SLOTS, slot).start()
+        return 0
+
+    lax.fori_loop(0, steps, step, 0)
+
+    uv_copy.wait()
+    for h in range(heads):
+        o = jnp.concatenate([ol[t, pl.ds(h, bsz, stride=heads), :] for t in range(lat // 128)], axis=1).astype(bf16)
+        oall[:, h * vh:(h + 1) * vh] = dot(o, uvbuf[h]).astype(bf16)
+    o_copy.wait()
+    h1 = (x_ref[...].astype(f32) + dot(oall[...], obuf[...])).astype(bf16)
+    h1_ref[...] = h1
+    h1 = h1.astype(f32)
+    u_ref[...] = (h1 * lax.rsqrt(jnp.mean(h1 * h1, axis=-1, keepdims=True) + EPS)).astype(bf16)
+
+
+def attention(x, cache, lens, w_q, w_dkv, w_uk, w_uv, w_o):
+    bsz, hid = x.shape
+    heads, nope, lat = w_uk.shape
+    rows, kvd = cache.shape[1:]
+    rot = kvd - lat
+    vh = w_uv.shape[2]
+    inv = ROPE_BASE ** (-2.0 * jnp.arange(rot // 2, dtype=jnp.float32) / rot)
+    ang = inv[:, None] * lens.astype(jnp.float32)[None, :]
+    tab = jnp.concatenate([jnp.cos(ang), jnp.sin(ang)], axis=0)
+    bf16, f32 = jnp.bfloat16, jnp.float32
+    vm = pl.BlockSpec(memory_space=pltpu.VMEM)
+    hbm = pl.BlockSpec(memory_space=pl.ANY)
+    dma = pltpu.SemaphoreType.DMA
+    wide = (kvd + 127) // 128 * 128
+    h1, u, kv = pl.pallas_call(
+        attn_kernel,
+        out_shape=(jax.ShapeDtypeStruct((bsz, hid), bf16), jax.ShapeDtypeStruct((bsz, hid), bf16),
+                   jax.ShapeDtypeStruct((kvd, bsz), bf16)),
+        in_specs=[pl.BlockSpec(memory_space=pltpu.SMEM), vm, vm] + [hbm] * 6,
+        out_specs=(vm, vm, vm),
+        scratch_shapes=[
+            pltpu.VMEM((CACHE_SLOTS, GROUP, kvd, rows), bf16),
+            pltpu.VMEM((Q_PARTS, hid, w_q.shape[1] // Q_PARTS), bf16),
+            pltpu.VMEM((kvd, hid), bf16),
+            pltpu.VMEM(w_uk.shape, bf16),
+            pltpu.VMEM(w_uv.shape, bf16),
+            pltpu.VMEM(w_o.shape, bf16),
+            pltpu.VMEM((wide // 128, bsz * heads, 128), f32),
+            pltpu.VMEM((bsz, wide), f32),
+            pltpu.VMEM((GROUP * heads, rows), f32),
+            pltpu.VMEM((lat // 128, bsz * heads, 128), f32),
+            pltpu.VMEM((bsz, heads * vh), bf16),
+            dma((CACHE_SLOTS,)), dma((Q_PARTS,)), dma((4,)),
+        ],
+        compiler_params=pltpu.CompilerParams(vmem_limit_bytes=67043328),
+        name='attn',
+    )(lens, x, tab, cache.transpose(0, 2, 1), w_q, w_dkv.T, w_uk, w_uv, w_o)
+    return h1, u, kv.T
 
 
 def moe_kernel(u_ref, h1_ref, meta_ref, sg, su, sd, eg, eu, ed, y_ref,
@@ -327,8 +452,7 @@
     exp_spec = P('ep', None, None)
 
     def local(x, cache, lens, ids, rw, w_q, w_dkv, w_uk, w_uv, w_o, s_gate, s_up, s_down, e_gate, e_up, e_down):
-        h1, kv_new = attention(x, cache, lens, w_q, w_dkv, w_uk, w_uv, w_o)
-        u = rms(h1).astype(jnp.bfloat16)
+        h1, u, kv_new = attention(x, cache, lens, w_q, w_dkv, w_uk, w_uv, w_o)
         meta = jnp.concatenate([jnp.pad(ids.astype(jnp.float32), ((0, 0), (0, 2))), jnp.pad(rw, ((0, 0), (0, 2)))], axis=1).T
         y = moe(u, h1, meta, s_gate, s_up, s_down, e_gate, e_up, e_down)
         return y, kv_new

time: 178 us -> 156 us (0.88)
  matrix products: 52.5 us -> 0 us
  Pallas kernels: 111 us -> 150 us
  local copies, waits for them, and re-layouts: 6.13 us -> 1.88 us
  other arithmetic: 7.2 us -> 3.4 us
    dot_general x7 -> x0, matrix products: 52.5 us -> none  [the longest x1 16.9 us: attention(): jnp.einsum('bhc,blc->bhl', qf, cache, preferred_element_type=jnp.float32)]
    pallas_call x0 -> x1, Pallas kernels: none -> 38.9 us  [attention(): pl.pallas_call(attn_kernel, out_shape=(jax.ShapeDtypeStruct((bsz, hid), b...]
    reduce_sum x3 -> x0, other arithmetic: 3.88 us -> none  [the longest x1 2.57 us: attention(): den = jnp.sum(e, axis=2) + e_new]
    unnamed x23 -> x1, local copies, waits for them, and re-layouts: 5.03 us -> 1.88 us
where the time goes in v2:
time: 156 us
  Pallas kernels  150 us (96%)
  other arithmetic  3.4 us (2%)
  local copies, waits for them, and re-layouts  1.88 us (1%)
    pallas_call x1, Pallas kernels, moe(): pl.pallas_call(moe_kernel, out_shape=jax.ShapeDtypeStruct((bsz, hid), bf1...  111 us
    pallas_call x1, Pallas kernels, attention(): pl.pallas_call(attn_kernel, out_shape=(jax.ShapeDtypeStruct((bsz, hid), b...  38.9 us

profile of v2, /device:TPU:0, one launch (start us, length us, event | category | flops | bytes accessed | tf_op | source)
XLA Modules:
  0.0 155.9 jit_solution(8511182871854252957)
XLA Ops:
  0.6 0.7 convert_element_type.9
  1.3 0.7 convert_element_type.10
  2.0 1.3 fusion.meta_ref
  3.3 0.1 multiply_cosine_fusion
  3.4 0.6 pad_maximum_fusion.tab_ref
  4.0 38.9 %attn.1 = (bf16[128,2048]{1,0:T(8,128)(2,1)}, bf16[128,2048]{1,0:T(8,128)(2,1)}, bf16[576,128]{1,0:T(8,128)(2,1)}) custom-call(s32[128]{0:T(128)} %lens_ref.1, bf16[128,2048]{1,0:T(8,128)(2,1)} %x_ref.1, f32[64,128]{1,0:T(8,128)} %pad_maximum_fusion.tab_ref, bf16[128,576,256]{2,1,0:T(8,128)(2,1)} %bitcast.6, bf16[2048,3072]{1,0:T(8,128)(2,1)} %wq.1, ...), custom_call_target="tpu_custom_call" | custom-call | tf_op jit(solution)/shard_map/attn/pallas_call | solution.py:167
  43.0 111.0 %moe.1 = bf16[128,2048]{1,0:T(8,128)(2,1)} custom-call(bf16[128,2048]{1,0:T(8,128)(2,1)} %get-tuple-element.5.u_ref, bf16[128,2048]{1,0:T(8,128)(2,1)} %get-tuple-element.6.h1_ref, f32[16,128]{1,0:T(8,128)} %fusion.meta_ref, bf16[2048,2816]{1,0:T(8,128)(2,1)} %sg.1, bf16[2048,2816]{1,0:T(8,128)(2,1)} %su.1, bf16[2,1408,2048]{2,1,0:T(8,128)(2,1)} %bitcast.7, ...), custom_call_target="tpu_custom_call" | custom-call | tf_op jit(solution)/shard_map/moe/pallas_call | solution.py:415
  154.0 1.9 %copy.19 = bf16[128,2048]{1,0:T(8,128)(2,1)} copy(bf16[128,2048]{1,0:T(8,128)(2,1)} %moe.1) | data formatting | bytes 1048576
  (1 shorter events, 0.0 us)
